TPU v7x, 32 devices: a whole 2x2x4 slice. The times are simulated.
32 devices in a mesh: groups: 2 (over x), seq: 16 (over z, y, core).
Axes of the slice: x: 2, y: 2, z: 4, core: 2. Of those that a mesh axis runs over, the one named last changes fastest.
Arguments:
- query_block: bfloat16 [512, 4096], P(('groups', 'seq')), parts along dimension 0, may hold values from -112 to 112
- cache_keys: bfloat16 [8192, 2048], P(('groups', 'seq')), parts along dimension 0, may hold values from -4 to 4
- stored_values: bfloat16 [8192, 2048], P(('groups', 'seq')), parts along dimension 0, may hold values from -6 to 6
- live_counts: int32 [32], P(('groups', 'seq')), parts along dimension 0, may hold values from 128 to 256
- first_position: int32 [2], P('groups'), parts along dimension 0, may hold values from 0 to 3840
- out_weight: bfloat16 [4096, 5376], P('seq'), may hold values from -0.09375 to 0.09375
Outputs:
- attended: bfloat16 [512, 5376], P(('groups', 'seq')), parts along dimension 0
There are 2 independent parts, one for each index of `groups`. A program takes and returns all parts, laid end to end along the dimension named above; an argument that names none is the same for every part. Nothing has to cross between parts.
Inputs may be any that keep to these rules, and one draw needn't show every extreme that they name: `live_counts`: the live slots of a block are its first ones.
All inputs are finite; a program needn't handle non-finite values.
Results may differ from a plain program's by a relative error of at most 0.0058.
Values may be sent and summed in bfloat16 or wider, within the bound.
No kernel may reach another device: no remote copies, remote signals or barrier semaphores. Data moves between devices by JAX's collectives and lax.ppermute only.
A program may use at most 64 MiB of HBM per device.

v0:
```python
import jax
import jax.numpy as jnp
from jax import lax
from jax.sharding import PartitionSpec as P

QUERY_HEADS = 32
KEY_VALUE_HEADS = 16
HEAD_SIZE = 128
score_scale = 168.0 ** (-0.5)
masked_value = -1e30


def head_partial(query_cols, key_cols, value_cols, allowed, group_width):
    row_count = query_cols.shape[0]
    grouped = query_cols.reshape(row_count, group_width, HEAD_SIZE)
    scores = (
        jnp.einsum("rgd,kd->grk", grouped, key_cols, preferred_element_type=jnp.float32)
        * score_scale
    )
    row_best = jnp.max(jnp.where(allowed[None], scores, masked_value), axis=2)
    shifted = jnp.where(allowed[None], scores - row_best[:, :, None], -jnp.inf)
    weights = jnp.exp(shifted)
    weight_sum = jnp.sum(weights, axis=2)
    safe_total = jnp.where(weight_sum > 0, weight_sum, 1.0)
    weighted = jnp.einsum(
        "grk,kd->grd", weights.astype(jnp.bfloat16), value_cols, preferred_element_type=jnp.float32
    )
    value_partial_sum = (weighted / safe_total[:, :, None]).astype(jnp.bfloat16)
    log_sum_exp = jnp.where(weight_sum > 0, row_best + jnp.log(safe_total), masked_value)
    return (value_partial_sum, log_sum_exp)


def merge_sources(received, totals):
    largest = jnp.max(totals, axis=0)
    scales = jnp.exp(totals - largest[None])
    blended = jnp.sum(scales[..., None] * received.astype(jnp.float32), axis=0)
    return (blended / jnp.sum(scales, axis=0)[..., None]).astype(jnp.bfloat16)


def body(query_block, cache_keys, stored_values, live_counts, first_position, out_weight):
    devices = lax.axis_size("seq")
    source = lax.axis_index("seq")
    key_count = cache_keys.shape[0]
    row_total = query_block.shape[0] * devices
    per_group = QUERY_HEADS // devices
    group_width = QUERY_HEADS // KEY_VALUE_HEADS
    first_key = source * key_count
    live_count = live_counts[0]
    begin_pos = first_position[0]
    key_index = lax.iota(jnp.int32, key_count)
    piece_rows = lax.all_gather(query_block, "seq", axis=0, tiled=True)
    row_count = piece_rows.shape[0]
    query_pos = begin_pos + lax.iota(jnp.int32, row_count)
    allowed = (key_index[None, :] < live_count) & (
        first_key + key_index[None, :] <= query_pos[:, None]
    )

    def single_head(key_value_head):
        query_cols = lax.dynamic_slice_in_dim(
            piece_rows, key_value_head * (group_width * HEAD_SIZE), group_width * HEAD_SIZE, 1
        )
        key_cols = lax.dynamic_slice_in_dim(cache_keys, key_value_head * HEAD_SIZE, HEAD_SIZE, 1)
        value_cols = lax.dynamic_slice_in_dim(
            stored_values, key_value_head * HEAD_SIZE, HEAD_SIZE, 1
        )
        return head_partial(query_cols, key_cols, value_cols, allowed, group_width)

    value_partial_sum, log_sum_exp = lax.map(
        single_head, jnp.arange(KEY_VALUE_HEADS, dtype=jnp.int32)
    )
    value_partial_sum = jnp.transpose(value_partial_sum, (2, 0, 1, 3)).reshape(
        row_count, QUERY_HEADS, HEAD_SIZE
    )
    log_sum_exp = jnp.transpose(log_sum_exp, (2, 0, 1)).reshape(row_count, QUERY_HEADS)
    value_partial_sum, log_sum_exp = (value_partial_sum, log_sum_exp)
    value_partial_sum, log_sum_exp = (value_partial_sum, log_sum_exp)
    received = lax.all_to_all(
        value_partial_sum[None], "seq", split_axis=2, concat_axis=0, tiled=True
    )
    totals = lax.all_to_all(log_sum_exp[None], "seq", split_axis=2, concat_axis=0, tiled=True)
    merged = merge_sources(received, totals)
    flattened = merged.reshape(row_total, per_group * HEAD_SIZE)
    summed = lax.psum_scatter(
        jnp.dot(flattened, out_weight, preferred_element_type=jnp.float32),
        "seq",
        scatter_dimension=0,
        tiled=True,
    )
    return summed.astype(jnp.bfloat16)


def solution(mesh):
    in_specs = (
        P(("groups", "seq"), None),
        P(("groups", "seq"), None),
        P(("groups", "seq"), None),
        P(("groups", "seq")),
        P("groups"),
        P("seq", None),
    )
    out_specs = P(("groups", "seq"), None)
    return jax.shard_map(body, mesh=mesh, in_specs=in_specs, out_specs=out_specs, check_vma=False)
```

profile of v0, /device:TPU:0, one launch (start us, length us, event | category | flops | bytes accessed | tf_op | source)
XLA Modules:
  0.0 307.4 jit_solution(6038253713847439832)
XLA Ops:
  8.7 45.0 %all-gather.2.cloned.1.call-done = bf16[256,4096]{1,0:T(8,128)(2,1)} async-done(((bf16[16,4096]{1,0:T(8,128)(2,1)}), bf16[256,4096]{1,0:T(8,128)(2,1)}) %all-gather.2.cloned.1.call-update) | async-done | bytes 2097168 | tf_op jit(solution)/shard_map/all_gather | solution.py:51
  53.7 97.2 %while.13 = (s32[]{:T(128)}, bf16[16,2,256,128]{3,2,1,0:T(8,128)(2,1)}, f32[16,2,256]{2,1,0:T(2,128)S(1)}, s32[16]{0:T(128)S(1)}, bf16[256,2048]{1,0:T(8,128)(2,...) while((s32[]{:T(128)}, ...), condition=%wide.region_3.4_spmd.clone, body=%wide.region_0.3_spmd.clone.sunk | while | flops 68552712 | bytes 2775577 | solution.py:68
  55.7 0.9 constant_dynamic-slice_fusion.2
  56.7 1.1 select_reduce_fusion.2
  58.0 1.8 fusion.40
  61.8 0.9 constant_dynamic-slice_fusion.2
  62.8 1.1 select_reduce_fusion.2
  64.0 1.8 fusion.40
  67.9 0.9 constant_dynamic-slice_fusion.2
  68.9 1.1 select_reduce_fusion.2
  70.1 1.8 fusion.40
  73.9 0.9 constant_dynamic-slice_fusion.2
  75.0 1.1 select_reduce_fusion.2
  76.2 1.8 fusion.40
  80.0 0.9 constant_dynamic-slice_fusion.2
  81.0 1.1 select_reduce_fusion.2
  82.3 1.8 fusion.40
  86.1 0.9 constant_dynamic-slice_fusion.2
  87.1 1.1 select_reduce_fusion.2
  88.3 1.8 fusion.40
  92.1 0.9 constant_dynamic-slice_fusion.2
  93.2 1.1 select_reduce_fusion.2
  94.4 1.8 fusion.40
  99.2 1.1 select_reduce_fusion.2
  100.5 1.8 fusion.40
  105.3 1.1 select_reduce_fusion.2
  106.6 1.8 fusion.40
  111.4 1.1 select_reduce_fusion.2
  112.6 1.8 fusion.40
  117.5 1.1 select_reduce_fusion.2
  118.7 1.8 fusion.40
  123.6 1.1 select_reduce_fusion.2
  124.8 1.8 fusion.40
  129.7 1.1 select_reduce_fusion.2
  130.9 1.8 fusion.40
  135.7 1.1 select_reduce_fusion.2
  136.9 1.8 fusion.40
  141.8 1.1 select_reduce_fusion.2
  143.0 1.8 fusion.40
  147.8 1.1 select_reduce_fusion.2
  149.1 1.8 fusion.40
  151.0 9.9 %all_to_all.27 = f32[1,256,32]{1,0,2:T(1,128)S(1)} all-to-all(f32[1,256,32]{1,0,2:T(1,128)S(1)} %broadcast_in_dim_reshape.6), channel_id=1, replica_groups=mesh['groups'=2,'seq'=16] {'seq'}, dimensions={2} | all-to-all | bytes 65536 | tf_op jit(solution)/shard_map/all_to_all | solution.py:80
  160.8 4.4 %all-to-all-start.1 = ((bf16[1,256,32,128]{3,1,0,2:T(8,128)(2,1)}), bf16[1,256,32,128]{3,1,0,2:T(8,128)(2,1)}, u32[]{:S(2)}, u32[]{:S(2)}) async-start(bf16[1,256,32,128]{3,1,0,2:T(8,128)(2,1)} %bitcast.71), calls=%async_computation.1 | async-start | bytes 4194304 | tf_op jit(solution)/shard_map/all_to_all | solution.py:77
  165.4 40.8 %all-to-all-done.1 = bf16[1,256,32,128]{3,1,0,2:T(8,128)(2,1)} async-done(((bf16[1,256,32,128]{3,1,0,2:T(8,128)(2,1)}), bf16[1,256,32,128]{3,1,0,2:T(8,128)(2,1)}, u32[]{:S(2)}, u32[]{:S(2)}) %all-to-all-start.1) | async-done | bytes 2097184 | tf_op jit(solution)/shard_map/all_to_all | solution.py:77
  206.2 2.5 fusion.22
  209.0 3.3 %fusion.26 = f32[256,5376]{1,0:T(8,128)} fusion(bf16[256,256]{0,1:T(8,128)(2,1)S(1)} %bitcast.72, bf16[256,5376]{1,0:T(8,128)(2,1)S(1)} %copy-done), kind=kOutput, calls=%fused_computation.39 | convolution fusion | flops 704643072 | bytes 8388608 | tf_op jit(solution)/shard_map/dot_general | solution.py:84
  212.4 86.6 %reduce-scatter.2.cloned.1.call-done = f32[16,5376]{1,0:T(8,128)} async-done(((f32[256,5376]{1,0:T(8,128)}), f32[16,5376]{1,0:T(8,128)}) %reduce-scatter.2.cloned.1.call-update) | async-done | bytes 344080 | tf_op jit(solution)/shard_map/reduce_scatter | solution.py:83
  298.9 1.7 convert_element_type.34
  (121 shorter events, 25.1 us)
Async XLA Ops:
  6.5 202.5 %copy-start = (bf16[256,5376]{1,0:T(8,128)(2,1)S(1)}, bf16[256,5376]{1,0:T(8,128)(2,1)}, u32[]{:S(2)}) copy-start(bf16[256,5376]{1,0:T(8,128)(2,1)} %param.13) | copy-start | bytes 8257540
  6.5 47.2 %all-gather.2.cloned.1.call-start = ((), (), s32[]{:S(2)}) async-start(), calls=%async_computation.3 | async-start | bytes 2228224 | tf_op jit(solution)/shard_map/all_gather | solution.py:51
  160.8 45.4 %all-to-all-start.1 = ((bf16[1,256,32,128]{3,1,0,2:T(8,128)(2,1)}), bf16[1,256,32,128]{3,1,0,2:T(8,128)(2,1)}, u32[]{:S(2)}, u32[]{:S(2)}) async-start(bf16[1,256,32,128]{3,1,0,2:T(8,128)(2,1)} %bitcast.71), calls=%async_computation.1 | async-start | bytes 4194304 | tf_op jit(solution)/shard_map/all_to_all | solution.py:77
  165.3 133.6 %reduce-scatter.2.cloned.1.call-start = ((), (), s32[]{:S(2)}) async-start(), calls=%async_computation.4 | async-start | bytes 5849088 | tf_op jit(solution)/shard_map/reduce_scatter | solution.py:83
Sparse Core Ops, SparseCore 0:
  9.5 44.1 all-gather.1
  212.5 86.3 reduce-scatter.1
where the time goes:
time: 310 us; the launch traced here: 307 us
  waiting for transfers between devices  173 us (56%)
  matrix products  49.7 us (16%)
  local copies, waits for them, and re-layouts  25.9 us (8%)
  loops' own time  20.5 us (7%)
  between operations  14.9 us (5%)
  blocking collectives  9.87 us (3%)
  other arithmetic  9 us (3%)
  starting transfers between devices  4.47 us (1%)
    reduce_scatter x1, waiting for transfers between devices, body(): lax.psum_scatter(jnp.dot(flattened, out_weight, preferred_element_type=jn...  86.6 us
    all_gather x1, waiting for transfers between devices, body(): piece_rows = lax.all_gather(query_block, 'seq', axis=0, tiled=True)  45 us
    all_to_all x1, waiting for transfers between devices, body(): lax.all_to_all(value_partial_sum[None], 'seq', split_axis=2, concat_axis=...  40.8 us
    dot_general x16, matrix products, head_partial(): jnp.einsum('grk,kd->grd', weights.astype(jnp.bfloat16), value_cols, prefe...  29.2 us
    another operation x1, loops' own time, body(): lax.map(single_head, jnp.arange(KEY_VALUE_HEADS, dtype=jnp.int32))  20.5 us
    dot_general x16, matrix products, head_partial(): jnp.einsum('rgd,kd->grk', grouped, key_cols, preferred_element_type=jnp.f...  17.1 us
    dynamic_slice x32, local copies, waits for them, and re-layouts, single_head(): lax.dynamic_slice_in_dim(piece_rows, key_value_head * (group_width * HEAD...  16.3 us
    all_to_all x1, blocking collectives, body(): lax.all_to_all(log_sum_exp[None], 'seq', split_axis=2, concat_axis=0, til...  9.87 us
  transfers between devices with their start and end apart: 3, of which 3 were waited for; matrix products, arithmetic and copies ran while one was open for 0% of the time, Pallas kernels for 0%

commit v1 on v0

--- a/solution.py
+++ b/solution.py
@@ -48,7 +48,12 @@
     live_count = live_counts[0]
     begin_pos = first_position[0]
     key_index = lax.iota(jnp.int32, key_count)
-    piece_rows = lax.all_gather(query_block, "seq", axis=0, tiled=True)
+    ring = [query_block]
+    for hop in range(15):
+        ring.append(lax.ppermute(ring[-1], "seq", [(dev, (dev + 1) % 16) for dev in range(16)]))
+    piece_rows = jnp.roll(
+        jnp.concatenate(ring[::-1], axis=0), (lax.axis_index("seq") + 1) * ring[0].shape[0], axis=0
+    )
     row_count = piece_rows.shape[0]
     query_pos = begin_pos + lax.iota(jnp.int32, row_count)
     allowed = (key_index[None, :] < live_count) & (

time: 310 us -> 401 us (1.29)
  waiting for transfers between devices: 173 us -> 234 us
  local copies, waits for them, and re-layouts: 25.9 us -> 45.4 us
  other arithmetic: 9 us -> 18.1 us
    ppermute x0 -> x15, waiting for transfers between devices: none -> 106 us  [body(): lax.ppermute(ring[-1], 'seq', [(dev, (dev + 1) % 16) for dev in range(16)])]
    all_gather x1 -> x0, waiting for transfers between devices: 45 us -> none  [body(): piece_rows = lax.all_gather(query_block, 'seq', axis=0, tiled=True)]
    unnamed x2 -> x67, local copies, waits for them, and re-layouts: 0.01 us -> 17.4 us
    dynamic_update_slice x16, other arithmetic: 0.3 us -> 9.48 us  [body(): lax.map(single_head, jnp.arange(KEY_VALUE_HEADS, dtype=jnp.int32))]
  transfers between devices with their start and end apart: 3 -> 17, of which waited for: 3 -> 17; matrix products, arithmetic and copies ran while one was open for 0% -> 0% of each run, Pallas kernels for 0% -> 0%
where the time goes in v1:
time: 401 us; the launch traced here: 398 us
  waiting for transfers between devices  234 us (58%)
  matrix products  49.8 us (12%)
  local copies, waits for them, and re-layouts  45.4 us (11%)
  loops' own time  21.5 us (5%)
  other arithmetic  18.1 us (5%)
  between operations  15.1 us (4%)
  blocking collectives  9.2 us (2%)
  starting transfers between devices  5 us (1%)
    ppermute x15, waiting for transfers between devices, body(): lax.ppermute(ring[-1], 'seq', [(dev, (dev + 1) % 16) for dev in range(16)])  106 us
    reduce_scatter x1, waiting for transfers between devices, body(): lax.psum_scatter(jnp.dot(flattened, out_weight, preferred_element_type=jn...  87 us
    all_to_all x1, waiting for transfers between devices, body(): lax.all_to_all(value_partial_sum[None], 'seq', split_axis=2, concat_axis=...  40.8 us
    dot_general x16, matrix products, head_partial(): jnp.einsum('grk,kd->grd', weights.astype(jnp.bfloat16), value_cols, prefe...  29.3 us
    another operation x1, loops' own time, body(): lax.map(single_head, jnp.arange(KEY_VALUE_HEADS, dtype=jnp.int32))  21.5 us
    unnamed x67, local copies, waits for them, and re-layouts  17.4 us
    dot_general x16, matrix products, head_partial(): jnp.einsum('rgd,kd->grk', grouped, key_cols, preferred_element_type=jnp.f...  17.2 us
    dynamic_slice x32, local copies, waits for them, and re-layouts, single_head(): lax.dynamic_slice_in_dim(piece_rows, key_value_head * (group_width * HEAD...  16.3 us
  transfers between devices with their start and end apart: 17, of which 17 were waited for; matrix products, arithmetic and copies ran while one was open for 0% of the time, Pallas kernels for 0%

profile of v1, /device:TPU:0, one launch (start us, length us, event | category | flops | bytes accessed | tf_op | source)
XLA Modules:
  0.0 398.1 jit_solution(10546637513717142564)
XLA Ops:
  7.0 7.9 %collective-permute-done = bf16[16,4096]{1,0:T(8,128)(2,1)S(1)} collective-permute-done((bf16[16,4096]{1,0:T(8,128)(2,1)}, bf16[16,4096]{1,0:T(8,128)(2,1)S(1)}, u32[]{:S(2)}, u32[]{:S(2)}) %collective-permute-start) | collective-permute-done | bytes 131104 | tf_op jit(solution)/shard_map/ppermute | solution.py:53
  14.9 7.1 %collective-permute-done.1 = bf16[16,4096]{1,0:T(8,128)(2,1)S(1)} collective-permute-done((bf16[16,4096]{1,0:T(8,128)(2,1)S(1)}, bf16[16,4096]{1,0:T(8,128)(2,1)S(1)}, u32[]{:S(2)}, u32[]{:S(2)}) %collective-permute-start.1) | collective-permute-done | bytes 131104 | tf_op jit(solution)/shard_map/ppermute | solution.py:53
  22.0 7.1 %collective-permute-done.2 = bf16[16,4096]{1,0:T(8,128)(2,1)S(1)} collective-permute-done((bf16[16,4096]{1,0:T(8,128)(2,1)S(1)}, bf16[16,4096]{1,0:T(8,128)(2,1)S(1)}, u32[]{:S(2)}, u32[]{:S(2)}) %collective-permute-start.2) | collective-permute-done | bytes 131104 | tf_op jit(solution)/shard_map/ppermute | solution.py:53
  29.1 7.1 %collective-permute-done.3 = bf16[16,4096]{1,0:T(8,128)(2,1)S(1)} collective-permute-done((bf16[16,4096]{1,0:T(8,128)(2,1)S(1)}, bf16[16,4096]{1,0:T(8,128)(2,1)S(1)}, u32[]{:S(2)}, u32[]{:S(2)}) %collective-permute-start.3) | collective-permute-done | bytes 131104 | tf_op jit(solution)/shard_map/ppermute | solution.py:53
  36.2 7.1 %collective-permute-done.4 = bf16[16,4096]{1,0:T(8,128)(2,1)S(1)} collective-permute-done((bf16[16,4096]{1,0:T(8,128)(2,1)S(1)}, bf16[16,4096]{1,0:T(8,128)(2,1)S(1)}, u32[]{:S(2)}, u32[]{:S(2)}) %collective-permute-start.4) | collective-permute-done | bytes 131104 | tf_op jit(solution)/shard_map/ppermute | solution.py:53
  43.3 7.1 %collective-permute-done.5 = bf16[16,4096]{1,0:T(8,128)(2,1)S(1)} collective-permute-done((bf16[16,4096]{1,0:T(8,128)(2,1)S(1)}, bf16[16,4096]{1,0:T(8,128)(2,1)S(1)}, u32[]{:S(2)}, u32[]{:S(2)}) %collective-permute-start.5) | collective-permute-done | bytes 131104 | tf_op jit(solution)/shard_map/ppermute | solution.py:53
  51.0 7.1 %collective-permute-done.6 = bf16[16,4096]{1,0:T(8,128)(2,1)S(1)} collective-permute-done((bf16[16,4096]{1,0:T(8,128)(2,1)S(1)}, bf16[16,4096]{1,0:T(8,128)(2,1)S(1)}, u32[]{:S(2)}, u32[]{:S(2)}) %collective-permute-start.6) | collective-permute-done | bytes 131104 | tf_op jit(solution)/shard_map/ppermute | solution.py:53
  58.7 7.1 %collective-permute-done.7 = bf16[16,4096]{1,0:T(8,128)(2,1)S(1)} collective-permute-done((bf16[16,4096]{1,0:T(8,128)(2,1)S(1)}, bf16[16,4096]{1,0:T(8,128)(2,1)S(1)}, u32[]{:S(2)}, u32[]{:S(2)}) %collective-permute-start.7) | collective-permute-done | bytes 131104 | tf_op jit(solution)/shard_map/ppermute | solution.py:53
  66.5 7.1 %collective-permute-done.8 = bf16[16,4096]{1,0:T(8,128)(2,1)S(1)} collective-permute-done((bf16[16,4096]{1,0:T(8,128)(2,1)S(1)}, bf16[16,4096]{1,0:T(8,128)(2,1)S(1)}, u32[]{:S(2)}, u32[]{:S(2)}) %collective-permute-start.8) | collective-permute-done | bytes 131104 | tf_op jit(solution)/shard_map/ppermute | solution.py:53
  74.2 7.1 %collective-permute-done.9 = bf16[16,4096]{1,0:T(8,128)(2,1)S(1)} collective-permute-done((bf16[16,4096]{1,0:T(8,128)(2,1)S(1)}, bf16[16,4096]{1,0:T(8,128)(2,1)S(1)}, u32[]{:S(2)}, u32[]{:S(2)}) %collective-permute-start.9) | collective-permute-done | bytes 131104 | tf_op jit(solution)/shard_map/ppermute | solution.py:53
  82.0 7.1 %collective-permute-done.10 = bf16[16,4096]{1,0:T(8,128)(2,1)S(1)} collective-permute-done((bf16[16,4096]{1,0:T(8,128)(2,1)S(1)}, bf16[16,4096]{1,0:T(8,128)(2,1)S(1)}, u32[]{:S(2)}, u32[]{:S(2)}) %collective-permute-start.10) | collective-permute-done | bytes 131104 | tf_op jit(solution)/shard_map/ppermute | solution.py:53
  89.7 7.1 %collective-permute-done.11 = bf16[16,4096]{1,0:T(8,128)(2,1)S(1)} collective-permute-done((bf16[16,4096]{1,0:T(8,128)(2,1)S(1)}, bf16[16,4096]{1,0:T(8,128)(2,1)S(1)}, u32[]{:S(2)}, u32[]{:S(2)}) %collective-permute-start.11) | collective-permute-done | bytes 131104 | tf_op jit(solution)/shard_map/ppermute | solution.py:53
  97.5 7.1 %collective-permute-done.12 = bf16[16,4096]{1,0:T(8,128)(2,1)S(1)} collective-permute-done((bf16[16,4096]{1,0:T(8,128)(2,1)S(1)}, bf16[16,4096]{1,0:T(8,128)(2,1)S(1)}, u32[]{:S(2)}, u32[]{:S(2)}) %collective-permute-start.12) | collective-permute-done | bytes 131104 | tf_op jit(solution)/shard_map/ppermute | solution.py:53
  105.9 6.5 %collective-permute-done.13 = bf16[16,4096]{1,0:T(8,128)(2,1)} collective-permute-done((bf16[16,4096]{1,0:T(8,128)(2,1)S(1)}, bf16[16,4096]{1,0:T(8,128)(2,1)}, u32[]{:S(2)}, u32[]{:S(2)}) %collective-permute-start.13) | collective-permute-done | bytes 131104 | tf_op jit(solution)/shard_map/ppermute | solution.py:53
  113.2 6.6 %collective-permute-done.14 = bf16[16,4096]{1,0:T(8,128)(2,1)} collective-permute-done((bf16[16,4096]{1,0:T(8,128)(2,1)}, bf16[16,4096]{1,0:T(8,128)(2,1)}, u32[]{:S(2)}, u32[]{:S(2)}) %collective-permute-start.14) | collective-permute-done | bytes 131104 | tf_op jit(solution)/shard_map/ppermute | solution.py:53
  132.2 1.5 constant_dynamic-slice_fusion.1
  133.7 107.3 %while.13 = (s32[]{:T(128)}, bf16[16,2,256,128]{3,2,1,0:T(8,128)(2,1)}, f32[16,2,256]{2,1,0:T(2,128)}, s32[16]{0:T(128)S(1)}, bf16[256,2048]{1,0:T(8,128)(2,1)},...) while((s32[]{:T(128)}, ...), condition=%wide.region_3.4_spmd.clone, body=%wide.region_0.3_spmd.clone.sunk | while | flops 68552712 | bytes 2776585 | solution.py:73
  138.0 1.8 fusion.40
  144.7 1.8 fusion.40
  150.2 1.1 select_reduce_fusion.2
  151.4 1.8 fusion.40
  158.1 1.8 fusion.40
  164.8 1.8 fusion.40
  170.3 1.1 select_reduce_fusion.2
  171.5 1.8 fusion.40
  178.2 1.8 fusion.40
  183.7 1.1 select_reduce_fusion.2
  184.9 1.8 fusion.40
  190.4 1.1 select_reduce_fusion.2
  191.7 1.8 fusion.40
  198.4 1.8 fusion.40
  203.9 1.1 select_reduce_fusion.2
  205.1 1.8 fusion.40
  210.6 1.1 select_reduce_fusion.2
  211.8 1.8 fusion.40
  217.3 1.1 select_reduce_fusion.2
  218.5 1.8 fusion.40
  225.2 1.8 fusion.40
  230.7 1.1 select_reduce_fusion.2
  231.9 1.8 fusion.40
  238.6 1.8 fusion.40
  241.8 9.2 %all_to_all.27 = f32[1,256,32]{1,0,2:T(1,128)S(1)} all-to-all(f32[1,256,32]{1,0,2:T(1,128)S(1)} %broadcast_in_dim_reshape.6), channel_id=1, replica_groups=mesh['groups'=2,'seq'=16] {'seq'}, dimensions={2} | all-to-all | bytes 65536 | tf_op jit(solution)/shard_map/all_to_all | solution.py:85
  251.0 4.4 %all-to-all-start.1 = ((bf16[1,256,32,128]{3,1,0,2:T(8,128)(2,1)}), bf16[1,256,32,128]{3,1,0,2:T(8,128)(2,1)}, u32[]{:S(2)}, u32[]{:S(2)}) async-start(bf16[1,256,32,128]{3,1,0,2:T(8,128)(2,1)} %bitcast.71), calls=%async_computation.1 | async-start | bytes 4194304 | tf_op jit(solution)/shard_map/all_to_all | solution.py:82
  255.6 40.8 %all-to-all-done.1 = bf16[1,256,32,128]{3,1,0,2:T(8,128)(2,1)} async-done(((bf16[1,256,32,128]{3,1,0,2:T(8,128)(2,1)}), bf16[1,256,32,128]{3,1,0,2:T(8,128)(2,1)}, u32[]{:S(2)}, u32[]{:S(2)}) %all-to-all-start.1) | async-done | bytes 2097184 | tf_op jit(solution)/shard_map/all_to_all | solution.py:82
  296.4 2.5 fusion.22
  299.2 3.3 fusion.26
  302.6 87.0 %reduce-scatter.2.cloned.1.call-done = f32[16,5376]{1,0:T(8,128)} async-done(((f32[256,5376]{1,0:T(8,128)}), f32[16,5376]{1,0:T(8,128)}) %reduce-scatter.2.cloned.1.call-update) | async-done | bytes 344080 | tf_op jit(solution)/shard_map/reduce_scatter | solution.py:88
  389.6 1.7 convert_element_type.34
  (215 shorter events, 67.0 us)
Async XLA Ops:
  6.5 292.7 %copy-start = (bf16[256,5376]{1,0:T(8,128)(2,1)S(1)}, bf16[256,5376]{1,0:T(8,128)(2,1)}, u32[]{:S(2)}) copy-start(bf16[256,5376]{1,0:T(8,128)(2,1)} %param.13) | copy-start | bytes 8257540
  6.5 125.7 %copy-start.1 = (bf16[16,4096]{1,0:T(8,128)(2,1)S(1)}, bf16[16,4096]{1,0:T(8,128)(2,1)}, u32[]{:S(2)}) copy-start(bf16[16,4096]{1,0:T(8,128)(2,1)} %param.8) | copy-start | bytes 393220
  6.5 8.4 %collective-permute-start = (bf16[16,4096]{1,0:T(8,128)(2,1)}, bf16[16,4096]{1,0:T(8,128)(2,1)S(1)}, u32[]{:S(2)}, u32[]{:S(2)}) collective-permute-start(bf16[16,4096]{1,0:T(8,128)(2,1)} %param.8), channel_id=1, source_target_pairs={{0,1},{1,2},{2,3},{3,4},{4,5},{5,6},{6,7},{7,8},{8,9},{9,10},{10,1... | collective-permute-start | bytes 393224 | tf_op jit(solution)/shard_map/ppermute | solution.py:53
  14.9 7.1 %collective-permute-start.1 = (bf16[16,4096]{1,0:T(8,128)(2,1)S(1)}, bf16[16,4096]{1,0:T(8,128)(2,1)S(1)}, u32[]{:S(2)}, u32[]{:S(2)}) collective-permute-start(bf16[16,4096]{1,0:T(8,128)(2,1)S(1)} %collective-permute-done), channel_id=1, source_target_pairs={{0,1},{1,2},{2,3},{3,4},{4,5},{5,6},{6,7},{7,8},{8,9},{9,10},{10,1... | collective-permute-start | bytes 393224 | tf_op jit(solution)/shard_map/ppermute | solution.py:53
  22.0 7.1 %collective-permute-start.2 = (bf16[16,4096]{1,0:T(8,128)(2,1)S(1)}, bf16[16,4096]{1,0:T(8,128)(2,1)S(1)}, u32[]{:S(2)}, u32[]{:S(2)}) collective-permute-start(bf16[16,4096]{1,0:T(8,128)(2,1)S(1)} %collective-permute-done.1), channel_id=1, source_target_pairs={{0,1},{1,2},{2,3},{3,4},{4,5},{5,6},{6,7},{7,8},{8,9},{9,10},{10,1... | collective-permute-start | bytes 393224 | tf_op jit(solution)/shard_map/ppermute | solution.py:53
  29.1 7.1 %collective-permute-start.3 = (bf16[16,4096]{1,0:T(8,128)(2,1)S(1)}, bf16[16,4096]{1,0:T(8,128)(2,1)S(1)}, u32[]{:S(2)}, u32[]{:S(2)}) collective-permute-start(bf16[16,4096]{1,0:T(8,128)(2,1)S(1)} %collective-permute-done.2), channel_id=1, source_target_pairs={{0,1},{1,2},{2,3},{3,4},{4,5},{5,6},{6,7},{7,8},{8,9},{9,10},{10,1... | collective-permute-start | bytes 393224 | tf_op jit(solution)/shard_map/ppermute | solution.py:53
  36.2 7.1 %collective-permute-start.4 = (bf16[16,4096]{1,0:T(8,128)(2,1)S(1)}, bf16[16,4096]{1,0:T(8,128)(2,1)S(1)}, u32[]{:S(2)}, u32[]{:S(2)}) collective-permute-start(bf16[16,4096]{1,0:T(8,128)(2,1)S(1)} %collective-permute-done.3), channel_id=1, source_target_pairs={{0,1},{1,2},{2,3},{3,4},{4,5},{5,6},{6,7},{7,8},{8,9},{9,10},{10,1... | collective-permute-start | bytes 393224 | tf_op jit(solution)/shard_map/ppermute | solution.py:53
  43.3 7.1 %collective-permute-start.5 = (bf16[16,4096]{1,0:T(8,128)(2,1)S(1)}, bf16[16,4096]{1,0:T(8,128)(2,1)S(1)}, u32[]{:S(2)}, u32[]{:S(2)}) collective-permute-start(bf16[16,4096]{1,0:T(8,128)(2,1)S(1)} %collective-permute-done.4), channel_id=1, source_target_pairs={{0,1},{1,2},{2,3},{3,4},{4,5},{5,6},{6,7},{7,8},{8,9},{9,10},{10,1... | collective-permute-start | bytes 393224 | tf_op jit(solution)/shard_map/ppermute | solution.py:53
  50.4 0.6 copy-start.2
  51.0 7.1 %collective-permute-start.6 = (bf16[16,4096]{1,0:T(8,128)(2,1)S(1)}, bf16[16,4096]{1,0:T(8,128)(2,1)S(1)}, u32[]{:S(2)}, u32[]{:S(2)}) collective-permute-start(bf16[16,4096]{1,0:T(8,128)(2,1)S(1)} %collective-permute-done.5), channel_id=1, source_target_pairs={{0,1},{1,2},{2,3},{3,4},{4,5},{5,6},{6,7},{7,8},{8,9},{9,10},{10,1... | collective-permute-start | bytes 393224 | tf_op jit(solution)/shard_map/ppermute | solution.py:53
  58.1 0.7 copy-start.4
  58.7 7.1 %collective-permute-start.7 = (bf16[16,4096]{1,0:T(8,128)(2,1)S(1)}, bf16[16,4096]{1,0:T(8,128)(2,1)S(1)}, u32[]{:S(2)}, u32[]{:S(2)}) collective-permute-start(bf16[16,4096]{1,0:T(8,128)(2,1)S(1)} %collective-permute-done.6), channel_id=1, source_target_pairs={{0,1},{1,2},{2,3},{3,4},{4,5},{5,6},{6,7},{7,8},{8,9},{9,10},{10,1... | collective-permute-start | bytes 393224 | tf_op jit(solution)/shard_map/ppermute | solution.py:53
  65.8 0.7 copy-start.6
  66.5 7.1 %collective-permute-start.8 = (bf16[16,4096]{1,0:T(8,128)(2,1)S(1)}, bf16[16,4096]{1,0:T(8,128)(2,1)S(1)}, u32[]{:S(2)}, u32[]{:S(2)}) collective-permute-start(bf16[16,4096]{1,0:T(8,128)(2,1)S(1)} %collective-permute-done.7), channel_id=1, source_target_pairs={{0,1},{1,2},{2,3},{3,4},{4,5},{5,6},{6,7},{7,8},{8,9},{9,10},{10,1... | collective-permute-start | bytes 393224 | tf_op jit(solution)/shard_map/ppermute | solution.py:53
  73.6 0.7 copy-start.8
  74.2 7.1 %collective-permute-start.9 = (bf16[16,4096]{1,0:T(8,128)(2,1)S(1)}, bf16[16,4096]{1,0:T(8,128)(2,1)S(1)}, u32[]{:S(2)}, u32[]{:S(2)}) collective-permute-start(bf16[16,4096]{1,0:T(8,128)(2,1)S(1)} %collective-permute-done.8), channel_id=1, source_target_pairs={{0,1},{1,2},{2,3},{3,4},{4,5},{5,6},{6,7},{7,8},{8,9},{9,10},{10,1... | collective-permute-start | bytes 393224 | tf_op jit(solution)/shard_map/ppermute | solution.py:53
  81.3 0.7 copy-start.10
  82.0 7.1 %collective-permute-start.10 = (bf16[16,4096]{1,0:T(8,128)(2,1)S(1)}, bf16[16,4096]{1,0:T(8,128)(2,1)S(1)}, u32[]{:S(2)}, u32[]{:S(2)}) collective-permute-start(bf16[16,4096]{1,0:T(8,128)(2,1)S(1)} %collective-permute-done.9), channel_id=1, source_target_pairs={{0,1},{1,2},{2,3},{3,4},{4,5},{5,6},{6,7},{7,8},{8,9},{9,10},{10,1... | collective-permute-start | bytes 393224 | tf_op jit(solution)/shard_map/ppermute | solution.py:53
  89.1 0.7 copy-start.12
  89.7 7.1 %collective-permute-start.11 = (bf16[16,4096]{1,0:T(8,128)(2,1)S(1)}, bf16[16,4096]{1,0:T(8,128)(2,1)S(1)}, u32[]{:S(2)}, u32[]{:S(2)}) collective-permute-start(bf16[16,4096]{1,0:T(8,128)(2,1)S(1)} %collective-permute-done.10), channel_id=1, source_target_pairs={{0,1},{1,2},{2,3},{3,4},{4,5},{5,6},{6,7},{7,8},{8,9},{9,10},{10,1... | collective-permute-start | bytes 393224 | tf_op jit(solution)/shard_map/ppermute | solution.py:53
  96.8 0.7 copy-start.14
  97.5 7.1 %collective-permute-start.12 = (bf16[16,4096]{1,0:T(8,128)(2,1)S(1)}, bf16[16,4096]{1,0:T(8,128)(2,1)S(1)}, u32[]{:S(2)}, u32[]{:S(2)}) collective-permute-start(bf16[16,4096]{1,0:T(8,128)(2,1)S(1)} %collective-permute-done.11), channel_id=1, source_target_pairs={{0,1},{1,2},{2,3},{3,4},{4,5},{5,6},{6,7},{7,8},{8,9},{9,10},{10,1... | collective-permute-start | bytes 393224 | tf_op jit(solution)/shard_map/ppermute | solution.py:53
  104.6 0.7 copy-start.16
  105.2 7.2 %collective-permute-start.13 = (bf16[16,4096]{1,0:T(8,128)(2,1)S(1)}, bf16[16,4096]{1,0:T(8,128)(2,1)}, u32[]{:S(2)}, u32[]{:S(2)}) collective-permute-start(bf16[16,4096]{1,0:T(8,128)(2,1)S(1)} %collective-permute-done.12), channel_id=1, source_target_pairs={{0,1},{1,2},{2,3},{3,4},{4,5},{5,6},{6,7},{7,8},{8,9},{9,10},{10,1... | collective-permute-start | bytes 393224 | tf_op jit(solution)/shard_map/ppermute | solution.py:53
  112.4 7.4 %collective-permute-start.14 = (bf16[16,4096]{1,0:T(8,128)(2,1)}, bf16[16,4096]{1,0:T(8,128)(2,1)}, u32[]{:S(2)}, u32[]{:S(2)}) collective-permute-start(bf16[16,4096]{1,0:T(8,128)(2,1)} %collective-permute-done.13), channel_id=1, source_target_pairs={{0,1},{1,2},{2,3},{3,4},{4,5},{5,6},{6,7},{7,8},{8,9},{9,10},{10,1... | collective-permute-start | bytes 393224 | tf_op jit(solution)/shard_map/ppermute | solution.py:53
  113.1 18.7 %copy-start.17 = (bf16[16,4096]{1,0:T(8,128)(2,1)S(1)}, bf16[16,4096]{1,0:T(8,128)(2,1)}, u32[]{:S(2)}) copy-start(bf16[16,4096]{1,0:T(8,128)(2,1)} %copy-done.16) | copy-start | bytes 393220
  113.1 18.8 %copy-start.15 = (bf16[16,4096]{1,0:T(8,128)(2,1)S(1)}, bf16[16,4096]{1,0:T(8,128)(2,1)}, u32[]{:S(2)}) copy-start(bf16[16,4096]{1,0:T(8,128)(2,1)} %copy-done.14) | copy-start | bytes 393220
  113.2 18.8 %copy-start.13 = (bf16[16,4096]{1,0:T(8,128)(2,1)S(1)}, bf16[16,4096]{1,0:T(8,128)(2,1)}, u32[]{:S(2)}) copy-start(bf16[16,4096]{1,0:T(8,128)(2,1)} %copy-done.12) | copy-start | bytes 393220
  113.2 18.8 %copy-start.11 = (bf16[16,4096]{1,0:T(8,128)(2,1)S(1)}, bf16[16,4096]{1,0:T(8,128)(2,1)}, u32[]{:S(2)}) copy-start(bf16[16,4096]{1,0:T(8,128)(2,1)} %copy-done.10) | copy-start | bytes 393220
  113.2 18.8 %copy-start.9 = (bf16[16,4096]{1,0:T(8,128)(2,1)S(1)}, bf16[16,4096]{1,0:T(8,128)(2,1)}, u32[]{:S(2)}) copy-start(bf16[16,4096]{1,0:T(8,128)(2,1)} %copy-done.8) | copy-start | bytes 393220
  113.2 18.8 %copy-start.7 = (bf16[16,4096]{1,0:T(8,128)(2,1)S(1)}, bf16[16,4096]{1,0:T(8,128)(2,1)}, u32[]{:S(2)}) copy-start(bf16[16,4096]{1,0:T(8,128)(2,1)} %copy-done.6) | copy-start | bytes 393220
  113.2 18.8 %copy-start.5 = (bf16[16,4096]{1,0:T(8,128)(2,1)S(1)}, bf16[16,4096]{1,0:T(8,128)(2,1)}, u32[]{:S(2)}) copy-start(bf16[16,4096]{1,0:T(8,128)(2,1)} %copy-done.4) | copy-start | bytes 393220
  113.2 18.9 %copy-start.3 = (bf16[16,4096]{1,0:T(8,128)(2,1)S(1)}, bf16[16,4096]{1,0:T(8,128)(2,1)}, u32[]{:S(2)}) copy-start(bf16[16,4096]{1,0:T(8,128)(2,1)} %copy-done.2) | copy-start | bytes 393220
  251.0 45.4 %all-to-all-start.1 = ((bf16[1,256,32,128]{3,1,0,2:T(8,128)(2,1)}), bf16[1,256,32,128]{3,1,0,2:T(8,128)(2,1)}, u32[]{:S(2)}, u32[]{:S(2)}) async-start(bf16[1,256,32,128]{3,1,0,2:T(8,128)(2,1)} %bitcast.71), calls=%async_computation.1 | async-start | bytes 4194304 | tf_op jit(solution)/shard_map/all_to_all | solution.py:82
  255.5 134.1 %reduce-scatter.2.cloned.1.call-start = ((), (), s32[]{:S(2)}) async-start(), calls=%async_computation.3 | async-start | bytes 5849088 | tf_op jit(solution)/shard_map/reduce_scatter | solution.py:88
Sparse Core Ops, SparseCore 0:
  302.7 86.8 reduce-scatter.1
